TPU v7x, 32 devices: a whole 2x2x4 slice. The times are simulated.
32 devices in a mesh: pipe: 4 (over y, core), vocab: 2 (over x), expert: 4 (over z).
Axes of the slice: x: 2, y: 2, z: 4, core: 2. Of those that a mesh axis runs over, the one named last changes fastest.
Arguments:
- token_ids: int32 [192], replicated, may hold values from 0 to 65535
- routes: int32 [192, 2], replicated, may hold values from 0 to 3, all different within a row; in each aligned block of 192 rows (0 to 191, 192 to 383, ...) at most 144 rows name the same one
- gate_weights: float32 [192, 2], replicated, may hold values from 0.2 to 1
- embed_table: bfloat16 [65536, 7168], P(('pipe', 'vocab'), 'expert'), may hold values from -0.59765625 to 0.59765625
- w_gate: bfloat16 [4, 7168, 2048], P('expert', None, ('pipe', 'vocab')), may hold values from -0.5 to 0.5
- w_up: bfloat16 [4, 7168, 2048], P('expert', None, ('pipe', 'vocab')), may hold values from -0.5 to 0.5
- w_down: bfloat16 [4, 2048, 7168], P('expert', ('pipe', 'vocab')), may hold values from -0.125 to 0.125
Outputs:
- logits: bfloat16 [192, 65536], P('expert', ('pipe', 'vocab'))
Inputs may be any that keep to these rules, and one draw needn't show every extreme that they name: `routes`: each row names 2 different experts; over all 192 rows no expert is named more than 144 times, a bound that some block reaches.
All inputs are finite; a program needn't handle non-finite values.
Results may differ from a plain program's by a relative error of at most 0.025.
Values may be sent and summed in bfloat16 or wider, within the bound.
A program may use at most 128 MiB of HBM per device.

v0:
```python
import jax
import jax.numpy as jnp
from jax import lax
from jax.sharding import PartitionSpec as P


def per_device(token_ids, routes, gate_weights, embed_table, w_gate, w_up, w_down):
    vocab_rows, width_cols = embed_table.shape
    tokens, top_count = routes.shape
    experts = lax.axis_size("expert")
    group_size = lax.axis_size(("pipe", "vocab"))
    capacity = group_size * (3 * tokens * top_count // (2 * experts * group_size))
    row_base = lax.axis_index(("pipe", "vocab")) * vocab_rows
    local_ids = token_ids - row_base
    in_shard = (local_ids >= 0) & (local_ids < vocab_rows)
    lookup_rows = jnp.take(embed_table, jnp.clip(local_ids, 0, vocab_rows - 1), axis=0)
    lookup_rows = jnp.where(in_shard[:, None], lookup_rows.astype(jnp.float32), 0.0)
    embedded = lax.psum(lookup_rows.astype(jnp.bfloat16), ("pipe", "vocab"))
    flat_routes = routes.reshape(-1)
    one_hot = (flat_routes[:, None] == jnp.arange(experts, dtype=jnp.int32)[None, :]).astype(
        jnp.int32
    )
    slot_index = jnp.sum((jnp.cumsum(one_hot, axis=0) - one_hot) * one_hot, axis=1)
    slot_dest = flat_routes * capacity + slot_index
    repeated = jnp.repeat(embedded, top_count, axis=0)
    buffer = jnp.zeros((experts * capacity, width_cols), jnp.bfloat16).at[slot_dest].set(repeated)
    buffer = buffer.reshape(experts, capacity, width_cols)
    flat_rows = lax.all_to_all(buffer, "expert", split_axis=0, concat_axis=2, tiled=True)[0]
    gate_proj = jnp.dot(flat_rows, w_gate[0], preferred_element_type=jnp.float32)
    up_proj = jnp.dot(flat_rows, w_up[0], preferred_element_type=jnp.float32)
    hidden = (jax.nn.silu(gate_proj) * up_proj).astype(jnp.bfloat16)
    partial_value = jnp.dot(hidden, w_down[0], preferred_element_type=jnp.float32)[None]
    shared = lax.psum_scatter(
        partial_value.astype(jnp.bfloat16), ("pipe", "vocab"), scatter_dimension=1, tiled=True
    ).astype(jnp.float32)
    shared = lax.all_to_all(
        shared.astype(jnp.bfloat16), "expert", split_axis=2, concat_axis=0, tiled=True
    ).astype(shared.dtype)
    returned = lax.all_gather(
        shared.astype(jnp.bfloat16), ("pipe", "vocab"), axis=1, tiled=True
    ).astype(shared.dtype)
    picked = returned.reshape(experts * capacity, width_cols)[slot_dest].reshape(
        tokens, top_count, width_cols
    )
    moe_out = jnp.sum(picked * gate_weights[:, :, None], axis=1)
    residual = (embedded.astype(jnp.float32) + moe_out).astype(jnp.bfloat16)
    return lax.psum_scatter(
        lax.dot_general(
            residual, embed_table, (((1,), (1,)), ((), ())), preferred_element_type=jnp.float32
        ).astype(jnp.bfloat16),
        "expert",
        scatter_dimension=0,
        tiled=True,
    )


def solution(mesh):
    return jax.shard_map(
        per_device,
        mesh=mesh,
        in_specs=(
            P(),
            P(),
            P(),
            P(("pipe", "vocab"), "expert"),
            P("expert", None, ("pipe", "vocab")),
            P("expert", None, ("pipe", "vocab")),
            P("expert", ("pipe", "vocab"), None),
        ),
        out_specs=P("expert", ("pipe", "vocab")),
        check_vma=False,
    )
```

profile of v0, /device:TPU:0, one launch (start us, length us, event | category | flops | bytes accessed | tf_op | source)
XLA Modules:
  0.0 428.2 jit_solution(8567750402209135640)
XLA Ops:
  6.5 0.7 compare_and_fusion
  7.2 14.9 %gather_fusion = bf16[192,1792]{1,0:T(8,128)(2,1)S(1)} fusion(bf16[8192,1792]{1,0:T(8,128)(2,1)} %param.10, s32[1024]{0:T(1024)S(1)} %pad_clamp_fusion.1), kind=kCustom, calls=%fused_computation | custom fusion | bytes 1377024 | tf_op jit(solution)/shard_map/jit(_take)/gather | solution.py:16
  22.1 1.2 select_convert_fusion
  23.8 1.2 reduce-window.6
  25.9 55.8 %all-reduce.4.cloned.1.call-done = bf16[192,1792]{1,0:T(8,128)(2,1)} async-done(((bf16[192,1792]{1,0:T(8,128)(2,1)}), bf16[192,1792]{1,0:T(8,128)(2,1)}) %all-reduce.4.cloned.1.call-update) | async-done | bytes 688144 | tf_op jit(solution)/shard_map/psum | solution.py:18
  81.6 1.8 broadcast_in_dim.42
  84.0 3.3 scatter_custom_fusion
  87.3 51.2 %all_to_all.33 = bf16[4,144,1792]{2,1,0:T(8,128)(2,1)S(1)} all-to-all(bf16[4,144,1792]{2,1,0:T(8,128)(2,1)S(1)} %bitcast.66), channel_id=1, replica_groups=mesh['pipe'=4,'vocab'=2,'expert'=4] {'expert'}, dimensions={0} | all-to-all | bytes 4128768 | tf_op jit(solution)/shard_map/all_to_all | solution.py:28
  138.5 1.1 copy.41
  139.8 1.8 copy-done
  141.6 0.8 fusion.5
  142.4 6.9 %fusion.1 = bf16[1,144,7168]{2,1,0:T(8,128)(2,1)} fusion(bf16[1,256,7168]{2,1,0:T(8,128)(2,1)} %param.13, bf16[144,7168]{1,0:T(8,128)(2,1)S(1)} %bitcast.63, bf16[1,7168,256]{2,1,0:T(8,128)(2,1)} %param.12, f32[144,256]{1,0:T(8,128)S(1)} %fusion.5), kind=kOutput, calls=%fused_computation.5 | convolution fusion | flops 1058217984 | bytes 11616256 | tf_op jit(solution)/shard_map/dot_general | solution.py:32
  149.2 58.3 %fusion = bf16[24,7168]{1,0:T(8,128)(2,1)S(1)} fusion(bf16[1,144,7168]{2,1,0:T(8,128)(2,1)} %fusion.1), kind=kCustom, calls=%all-reduce-scatter | all-reduce-scatter fusion | flops 1376257 | bytes 2408960
  207.6 1.9 collective-permute-start
  209.6 1.7 collective-permute-start.1
  212.6 4.5 %collective-permute-done = bf16[24,7168]{1,0:T(8,128)(2,1)S(1)} collective-permute-done((bf16[24,7168]{1,0:T(8,128)(2,1)S(1)}, bf16[24,7168]{1,0:T(8,128)(2,1)S(1)}, u32[]{:S(2)}, u32[]{:S(2)}) %collective-permute-start) | collective-permute-done | bytes 344096
  217.0 4.8 %concatenate = bf16[66,7168]{1,0:T(8,128)(2,1)S(1)} concatenate(bf16[18,7168]{1,0:T(8,128)(2,1)S(1)} %collective-permute-done.1, bf16[24,7168]{1,0:T(8,128)(2,1)S(1)} %collective-permute-done, bf16[24,7168]{1,0:T(8,128)(2,1)S(1)} %fusion), dimensions={0} | concatenate | bytes 1892352
  222.0 6.0 %copy.42 = bf16[1,18,7168]{1,0,2:T(2,128)(2,1)} copy(bf16[1,18,7168]{2,1,0:T(8,128)(2,1)S(1)} %dynamic-slice_bitcast_fusion) | data formatting | bytes 516096 | tf_op jit(solution)/shard_map/reduce_scatter | solution.py:33
  228.5 39.8 %reduce.4 = bf16[7168,18]{1,0:T(8,128)(2,1)S(1)} reduce(bf16[7168,1,18]{2,1,0:T(2,128)(2,1)} %bitcast.64, bf16[]{:T(256)} %broadcast.68), dimensions={1}, to_apply=%bitcast.56.reduce_sub_computation | reduce | bytes 516098
  268.3 3.4 reshape.114
  271.7 9.8 %all_to_all.34 = bf16[4,2,16128]{2,1,0:T(2,128)(2,1)S(1)} all-to-all(bf16[4,2,16128]{2,1,0:T(2,128)(2,1)S(1)} %reshape.114), channel_id=1, replica_groups=mesh['pipe'=4,'vocab'=2,'expert'=4] {'expert'}, dimensions={0} | all-to-all | bytes 516096 | tf_op jit(solution)/shard_map/all_to_all | solution.py:36
  281.4 5.2 %reshape.115 = bf16[7168,1,18]{2,1,0:T(2,128)(2,1)} reshape(bf16[4,2,16128]{2,1,0:T(2,128)(2,1)S(1)} %all_to_all.34) | data formatting | bytes 516096
  286.6 7.3 %copy.43 = bf16[1,18,7168]{2,1,0:T(8,128)(2,1)S(1)} copy(bf16[1,18,7168]{1,0,2:T(2,128)(2,1)} %bitcast.65) | data formatting | bytes 516096 | tf_op jit(solution)/shard_map/all_to_all | solution.py:36
  293.9 0.8 all_to_all.28
  295.1 29.7 %all-gather.3.cloned.1.call-done = bf16[4,1,144,1792]{3,0,1,2:T(4,128)(2,1)} async-done(((bf16[4,1,18,1792]{3,0,1,2:T(4,128)(2,1)}), bf16[4,1,144,1792]{3,0,1,2:T(4,128)(2,1)}) %all-gather.3.cloned.1.call-update) | async-done | bytes 2064400 | tf_op jit(solution)/shard_map/all_gather | solution.py:39
  324.8 1.8 copy.45
  326.6 2.4 bitcast_convert_fusion
  329.0 6.1 %gather_fusion.1 = f32[384,1792]{1,0:T(8,128)S(1)} fusion(f32[576,1792]{1,0:T(8,128)} %bitcast_convert_fusion, s32[1024]{0:T(1024)S(1)} %pad_clamp_fusion), kind=kCustom, calls=%fused_computation.1 | custom fusion | bytes 5506560 | tf_op jit(solution)/shard_map/gather | solution.py:42
  335.1 2.8 reshape.75
  337.8 5.9 %multiply_reduce_fusion = f32[192,1792]{1,0:T(8,128)S(1)} fusion(f32[192,2,1792]{2,1,0:T(2,128)} %reshape.75, f32[192,2]{1,0:T(8,128)S(1)} %copy.46), kind=kLoop, calls=%fused_computation.11 | loop fusion | flops 1032192 | bytes 4130304 | tf_op jit(solution)/shard_map/reduce_sum | solution.py:45
  343.8 17.4 %convolution_convert_fusion = bf16[192,8192]{1,0:T(8,128)(2,1)} fusion(bf16[8192,1792]{1,0:T(8,128)(2,1)} %param.10, f32[192,1792]{1,0:T(8,128)S(1)} %multiply_reduce_fusion, bf16[192,1792]{1,0:T(8,128)(2,1)S(1)} %copy-done.1), kind=kOutput, calls=%fused_computation.3 | convolution fusion | flops 5639749632 | bytes 34570240 | tf_op jit(solution)/shard_map/dot_general | solution.py:48
  361.1 60.6 %reduce-scatter.5.cloned.1.call-done = bf16[48,8192]{1,0:T(8,128)(2,1)} async-done(((bf16[192,8192]{1,0:T(8,128)(2,1)}), bf16[48,8192]{1,0:T(8,128)(2,1)}) %reduce-scatter.5.cloned.1.call-update) | async-done | bytes 786448 | tf_op jit(solution)/shard_map/reduce_scatter | solution.py:47
  (37 shorter events, 3.8 us)
Async XLA Ops:
  6.5 75.1 %all-reduce.4.cloned.1.call-start = ((), (), s32[]{:S(2)}) async-start(), calls=%async_computation.3 | async-start | bytes 1376256 | tf_op jit(solution)/shard_map/psum | solution.py:18
  22.1 1.3 copy-start.2
  23.3 301.5 %all-gather.3.cloned.1.call-start = ((), (), s32[]{:S(2)}) async-start(), calls=%async_computation.5 | async-start | bytes 2322432 | tf_op jit(solution)/shard_map/all_gather | solution.py:39
  139.5 2.0 copy-start
  149.2 62.1 %copy-start.4 = (u32[32]{0:T(128)S(1)}, u32[32]{0:T(128)}, u32[]{:S(2)}) copy-start(u32[32]{0:T(128)} %constant.54) | copy-start | bytes 388
  207.6 9.5 %collective-permute-start = (bf16[24,7168]{1,0:T(8,128)(2,1)S(1)}, bf16[24,7168]{1,0:T(8,128)(2,1)S(1)}, u32[]{:S(2)}, u32[]{:S(2)}) collective-permute-start(bf16[24,7168]{1,0:T(8,128)(2,1)S(1)} %fusion), channel_id=1, source_target_pairs={{0,4},{4,8},{8,12},{12,16},{16,20},{20,24},{24,28},{1,5},{5,9},{9,... | collective-permute-start | bytes 1032200
  209.6 3.0 collective-permute-start.1
  286.6 8.4 %copy-start.3 = (f32[192,2]{0,1:T(2,128)S(1)}, f32[192,2]{0,1:T(2,128)}, u32[]{:S(2)}) copy-start(f32[192,2]{0,1:T(2,128)} %param.9) | copy-start | bytes 4612
  294.7 127.0 %reduce-scatter.5.cloned.1.call-start = ((), (), s32[]{:S(2)}) async-start(), calls=%async_computation.4 | async-start | bytes 3932160 | tf_op jit(solution)/shard_map/reduce_scatter | solution.py:47
  337.8 5.9 %copy-start.1 = (bf16[192,1792]{1,0:T(8,128)(2,1)S(1)}, bf16[192,1792]{1,0:T(8,128)(2,1)}, u32[]{:S(2)}) copy-start(bf16[192,1792]{1,0:T(8,128)(2,1)} %all-reduce.4.cloned.1.call-done) | copy-start | bytes 2064388
Sparse Core Ops, SparseCore 0:
  23.5 58.1 all-reduce.3
  294.8 29.9 all-gather.2
  361.3 60.3 reduce-scatter.4
where the time goes:
time: 429 us; the launch traced here: 428 us
  waiting for transfers between devices  151 us (35%)
  blocking collectives  119 us (28%)
  local copies, waits for them, and re-layouts  64 us (15%)
  other arithmetic  51.5 us (12%)
  matrix products  25 us (6%)
  between operations  14 us (3%)
    reduce_scatter x1, waiting for transfers between devices, per_device(): lax.psum_scatter(lax.dot_general(residual, embed_table, (((1,), (1,)), ((...  60.6 us
    unnamed x1, blocking collectives  58.3 us
    psum x1, waiting for transfers between devices, per_device(): embedded = lax.psum(lookup_rows.astype(jnp.bfloat16), ('pipe', 'vocab'))  55.8 us
    all_to_all x1, blocking collectives, per_device(): lax.all_to_all(buffer, 'expert', split_axis=0, concat_axis=2, tiled=True)[0]  51.2 us
    unnamed x2, other arithmetic  39.8 us
    all_gather x1, waiting for transfers between devices, per_device(): lax.all_gather(shared.astype(jnp.bfloat16), ('pipe', 'vocab'), axis=1, ti...  29.7 us
    dot_general x1, matrix products, per_device(): lax.dot_general(residual, embed_table, (((1,), (1,)), ((), ())), preferre...  17.4 us
    unnamed x20, local copies, waits for them, and re-layouts  16.9 us
  transfers between devices with their start and end apart: 5, of which 4 were waited for; matrix products, arithmetic and copies ran while one was open for 1% of the time, Pallas kernels for 0%

commit v1 on v0

--- a/solution.py
+++ b/solution.py
@@ -15,7 +15,7 @@
     in_shard = (local_ids >= 0) & (local_ids < vocab_rows)
     lookup_rows = jnp.take(embed_table, jnp.clip(local_ids, 0, vocab_rows - 1), axis=0)
     lookup_rows = jnp.where(in_shard[:, None], lookup_rows.astype(jnp.float32), 0.0)
-    embedded = lax.psum(lookup_rows.astype(jnp.bfloat16), ("pipe", "vocab"))
+    embedded = lax.psum(lax.psum(lookup_rows.astype(jnp.bfloat16), "pipe"), "vocab")
     flat_routes = routes.reshape(-1)
     one_hot = (flat_routes[:, None] == jnp.arange(experts, dtype=jnp.int32)[None, :]).astype(
         jnp.int32

time: 429 us -> 443 us (1.033)
  waiting for transfers between devices: 151 us -> 164 us
    psum x1 -> x2, waiting for transfers between devices: 55.8 us -> 69 us  [the longest x1 35.5 us: per_device(): lax.psum(lookup_rows.astype(jnp.bfloat16), 'pipe')]
  transfers between devices with their start and end apart: 5 -> 6, of which waited for: 4 -> 5; matrix products, arithmetic and copies ran while one was open for 1% -> 1% of each run, Pallas kernels for 0% -> 0%
where the time goes in v1:
time: 443 us
  waiting for transfers between devices  164 us (37%)
  blocking collectives  120 us (27%)
  local copies, waits for them, and re-layouts  64 us (14%)
  other arithmetic  51.5 us (12%)
  matrix products  25 us (6%)
  between operations  14 us (3%)
    reduce_scatter x1, waiting for transfers between devices, per_device(): lax.psum_scatter(lax.dot_general(residual, embed_table, (((1,), (1,)), ((...  60.6 us
    unnamed x1, blocking collectives  58 us
    all_to_all x1, blocking collectives, per_device(): lax.all_to_all(buffer, 'expert', split_axis=0, concat_axis=2, tiled=True)[0]  51.7 us
    unnamed x2, other arithmetic  39.8 us
    psum x1, waiting for transfers between devices, per_device(): lax.psum(lookup_rows.astype(jnp.bfloat16), 'pipe')  35.5 us
    psum x1, waiting for transfers between devices, per_device(): lax.psum(lax.psum(lookup_rows.astype(jnp.bfloat16), 'pipe'), 'vocab')  33.5 us
    all_gather x1, waiting for transfers between devices, per_device(): lax.all_gather(shared.astype(jnp.bfloat16), ('pipe', 'vocab'), axis=1, ti...  30.2 us
    dot_general x1, matrix products, per_device(): lax.dot_general(residual, embed_table, (((1,), (1,)), ((), ())), preferre...  17.3 us
  transfers between devices with their start and end apart: 6, of which 5 were waited for; matrix products, arithmetic and copies ran while one was open for 1% of the time, Pallas kernels for 0%

profile of v1, /device:TPU:0, one launch (start us, length us, event | category | flops | bytes accessed | tf_op | source)
XLA Modules:
  0.0 442.6 jit_solution(166587048812645597)
XLA Ops:
  7.2 14.9 %gather_fusion = bf16[192,1792]{1,0:T(8,128)(2,1)S(1)} fusion(bf16[8192,1792]{1,0:T(8,128)(2,1)} %param.10, s32[1024]{0:T(1024)S(1)} %pad_clamp_fusion.1), kind=kCustom, calls=%fused_computation | custom fusion | bytes 1377024 | tf_op jit(solution)/shard_map/jit(_take)/gather | solution.py:16
  22.1 1.2 select_convert_fusion
  23.7 1.2 reduce-window.6
  24.9 35.5 %all-reduce.5.cloned.1.call-done = bf16[192,1792]{1,0:T(8,128)(2,1)} async-done(((bf16[192,1792]{1,0:T(8,128)(2,1)}), bf16[192,1792]{1,0:T(8,128)(2,1)}) %all-reduce.5.cloned.1.call-update) | async-done | bytes 688144 | tf_op jit(solution)/shard_map/psum | solution.py:18
  61.4 33.5 %all-reduce.7.cloned.1.call-done = bf16[192,1792]{1,0:T(8,128)(2,1)} async-done(((bf16[192,1792]{1,0:T(8,128)(2,1)}), bf16[192,1792]{1,0:T(8,128)(2,1)}) %all-reduce.7.cloned.1.call-update) | async-done | bytes 688144 | tf_op jit(solution)/shard_map/psum | solution.py:18
  95.0 1.8 broadcast_in_dim.42
  97.3 3.3 scatter_custom_fusion
  100.6 51.7 %all_to_all.33 = bf16[4,144,1792]{2,1,0:T(8,128)(2,1)S(1)} all-to-all(bf16[4,144,1792]{2,1,0:T(8,128)(2,1)S(1)} %bitcast.66), channel_id=1, replica_groups=mesh['pipe'=4,'vocab'=2,'expert'=4] {'expert'}, dimensions={0} | all-to-all | bytes 4128768 | tf_op jit(solution)/shard_map/all_to_all | solution.py:28
  152.3 1.1 copy.41
  153.7 1.8 copy-done
  155.5 0.8 fusion.5
  156.3 6.9 %fusion.1 = bf16[1,144,7168]{2,1,0:T(8,128)(2,1)} fusion(bf16[1,256,7168]{2,1,0:T(8,128)(2,1)} %param.13, bf16[144,7168]{1,0:T(8,128)(2,1)S(1)} %bitcast.63, bf16[1,7168,256]{2,1,0:T(8,128)(2,1)} %param.12, f32[144,256]{1,0:T(8,128)S(1)} %fusion.5), kind=kOutput, calls=%fused_computation.5 | convolution fusion | flops 1058217984 | bytes 11616256 | tf_op jit(solution)/shard_map/dot_general | solution.py:32
  163.1 58.0 %fusion = bf16[24,7168]{1,0:T(8,128)(2,1)S(1)} fusion(bf16[1,144,7168]{2,1,0:T(8,128)(2,1)} %fusion.1), kind=kCustom, calls=%all-reduce-scatter | all-reduce-scatter fusion | flops 1376257 | bytes 2408960
  221.2 2.2 collective-permute-start
  223.5 1.7 collective-permute-start.1
  226.5 4.5 %collective-permute-done = bf16[24,7168]{1,0:T(8,128)(2,1)S(1)} collective-permute-done((bf16[24,7168]{1,0:T(8,128)(2,1)S(1)}, bf16[24,7168]{1,0:T(8,128)(2,1)S(1)}, u32[]{:S(2)}, u32[]{:S(2)}) %collective-permute-start) | collective-permute-done | bytes 344096
  230.9 4.8 %concatenate = bf16[66,7168]{1,0:T(8,128)(2,1)S(1)} concatenate(bf16[18,7168]{1,0:T(8,128)(2,1)S(1)} %collective-permute-done.1, bf16[24,7168]{1,0:T(8,128)(2,1)S(1)} %collective-permute-done, bf16[24,7168]{1,0:T(8,128)(2,1)S(1)} %fusion), dimensions={0} | concatenate | bytes 1892352
  235.9 6.0 %copy.42 = bf16[1,18,7168]{1,0,2:T(2,128)(2,1)} copy(bf16[1,18,7168]{2,1,0:T(8,128)(2,1)S(1)} %dynamic-slice_bitcast_fusion) | data formatting | bytes 516096 | tf_op jit(solution)/shard_map/reduce_scatter | solution.py:33
  242.4 39.8 %reduce.4 = bf16[7168,18]{1,0:T(8,128)(2,1)S(1)} reduce(bf16[7168,1,18]{2,1,0:T(2,128)(2,1)} %bitcast.64, bf16[]{:T(256)} %broadcast.68), dimensions={1}, to_apply=%bitcast.56.reduce_sub_computation | reduce | bytes 516098
  282.2 3.4 reshape.114
  285.6 9.7 %all_to_all.34 = bf16[4,2,16128]{2,1,0:T(2,128)(2,1)S(1)} all-to-all(bf16[4,2,16128]{2,1,0:T(2,128)(2,1)S(1)} %reshape.114), channel_id=1, replica_groups=mesh['pipe'=4,'vocab'=2,'expert'=4] {'expert'}, dimensions={0} | all-to-all | bytes 516096 | tf_op jit(solution)/shard_map/all_to_all | solution.py:36
  295.3 5.2 %reshape.115 = bf16[7168,1,18]{2,1,0:T(2,128)(2,1)} reshape(bf16[4,2,16128]{2,1,0:T(2,128)(2,1)S(1)} %all_to_all.34) | data formatting | bytes 516096
  300.5 7.3 %copy.43 = bf16[1,18,7168]{2,1,0:T(8,128)(2,1)S(1)} copy(bf16[1,18,7168]{1,0,2:T(2,128)(2,1)} %bitcast.65) | data formatting | bytes 516096 | tf_op jit(solution)/shard_map/all_to_all | solution.py:36
  307.8 0.8 all_to_all.28
  309.0 30.2 %all-gather.3.cloned.1.call-done = bf16[4,1,144,1792]{3,0,1,2:T(4,128)(2,1)} async-done(((bf16[4,1,18,1792]{3,0,1,2:T(4,128)(2,1)}), bf16[4,1,144,1792]{3,0,1,2:T(4,128)(2,1)}) %all-gather.3.cloned.1.call-update) | async-done | bytes 2064400 | tf_op jit(solution)/shard_map/all_gather | solution.py:39
  339.2 1.8 copy.45
  341.0 2.4 bitcast_convert_fusion
  343.3 6.1 %gather_fusion.1 = f32[384,1792]{1,0:T(8,128)S(1)} fusion(f32[576,1792]{1,0:T(8,128)} %bitcast_convert_fusion, s32[1024]{0:T(1024)S(1)} %pad_clamp_fusion), kind=kCustom, calls=%fused_computation.1 | custom fusion | bytes 5506560 | tf_op jit(solution)/shard_map/gather | solution.py:42
  349.4 2.8 reshape.75
  352.2 5.9 %multiply_reduce_fusion = f32[192,1792]{1,0:T(8,128)S(1)} fusion(f32[192,2,1792]{2,1,0:T(2,128)} %reshape.75, f32[192,2]{1,0:T(8,128)S(1)} %copy.46), kind=kLoop, calls=%fused_computation.11 | loop fusion | flops 1032192 | bytes 4130304 | tf_op jit(solution)/shard_map/reduce_sum | solution.py:45
  358.1 17.3 %convolution_convert_fusion = bf16[192,8192]{1,0:T(8,128)(2,1)} fusion(bf16[8192,1792]{1,0:T(8,128)(2,1)} %param.10, f32[192,1792]{1,0:T(8,128)S(1)} %multiply_reduce_fusion, bf16[192,1792]{1,0:T(8,128)(2,1)S(1)} %copy-done.1), kind=kOutput, calls=%fused_computation.3 | convolution fusion | flops 5639749632 | bytes 34570240 | tf_op jit(solution)/shard_map/dot_general | solution.py:48
  375.5 60.6 %reduce-scatter.5.cloned.1.call-done = bf16[48,8192]{1,0:T(8,128)(2,1)} async-done(((bf16[192,8192]{1,0:T(8,128)(2,1)}), bf16[48,8192]{1,0:T(8,128)(2,1)}) %reduce-scatter.5.cloned.1.call-update) | async-done | bytes 786448 | tf_op jit(solution)/shard_map/reduce_scatter | solution.py:47
  (40 shorter events, 4.5 us)
Async XLA Ops:
  6.5 53.9 %all-reduce.5.cloned.1.call-start = ((), (), s32[]{:S(2)}) async-start(), calls=%async_computation.3 | async-start | bytes 1376256 | tf_op jit(solution)/shard_map/psum | solution.py:18
  22.1 1.3 copy-start.2
  23.3 71.6 %all-reduce.7.cloned.1.call-start = ((), (), s32[]{:S(2)}) async-start(), calls=%async_computation.4 | async-start | bytes 1376256 | tf_op jit(solution)/shard_map/psum | solution.py:18
  60.4 278.8 %all-gather.3.cloned.1.call-start = ((), (), s32[]{:S(2)}) async-start(), calls=%async_computation.6 | async-start | bytes 2322432 | tf_op jit(solution)/shard_map/all_gather | solution.py:39
  153.4 2.0 copy-start
  163.1 62.1 %copy-start.4 = (u32[32]{0:T(128)S(1)}, u32[32]{0:T(128)}, u32[]{:S(2)}) copy-start(u32[32]{0:T(128)} %constant.54) | copy-start | bytes 388
  221.2 9.8 %collective-permute-start = (bf16[24,7168]{1,0:T(8,128)(2,1)S(1)}, bf16[24,7168]{1,0:T(8,128)(2,1)S(1)}, u32[]{:S(2)}, u32[]{:S(2)}) collective-permute-start(bf16[24,7168]{1,0:T(8,128)(2,1)S(1)} %fusion), channel_id=1, source_target_pairs={{0,4},{4,8},{8,12},{12,16},{16,20},{20,24},{24,28},{1,5},{5,9},{9,... | collective-permute-start | bytes 1032200
  223.5 3.0 collective-permute-start.1
  300.5 8.4 %copy-start.3 = (f32[192,2]{0,1:T(2,128)S(1)}, f32[192,2]{0,1:T(2,128)}, u32[]{:S(2)}) copy-start(f32[192,2]{0,1:T(2,128)} %param.9) | copy-start | bytes 4612
  308.6 127.4 %reduce-scatter.5.cloned.1.call-start = ((), (), s32[]{:S(2)}) async-start(), calls=%async_computation.5 | async-start | bytes 3932160 | tf_op jit(solution)/shard_map/reduce_scatter | solution.py:47
  352.2 5.9 %copy-start.1 = (bf16[192,1792]{1,0:T(8,128)(2,1)S(1)}, bf16[192,1792]{1,0:T(8,128)(2,1)}, u32[]{:S(2)}) copy-start(bf16[192,1792]{1,0:T(8,128)(2,1)} %all-reduce.7.cloned.1.call-done) | copy-start | bytes 2064388
Sparse Core Ops, SparseCore 0:
  23.5 36.8 all-reduce.4
  62.7 32.2 all-reduce.6
  308.7 30.4 all-gather.2
  375.6 60.3 reduce-scatter.4
